TPU v7x, 32 devices: a whole 2x2x4 slice. The times are simulated.
32 devices in a mesh: rows: 16 (over z, y, x), cols: 2 (over core).
Axes of the slice: x: 2, y: 2, z: 4, core: 2. Of those that a mesh axis runs over, the one named last changes fastest.
Arguments:
- design: float32 [16384, 512], P('rows', 'cols'), may hold values from -24 to 24
- signs: int32 [16384], P('rows'), may hold values from -1 to 1, as said below
- kept: int32 [1024], replicated, may hold values from 0 to 16383, as said below
Outputs:
- sketch: float32 [1024, 512], P('rows', 'cols')
- factor: float32 [512, 512], P(None, 'cols')
Inputs may be any that keep to these rules, and one draw needn't show every extreme that they name: `signs`: each entry is +1 or -1. `kept`: distinct and increasing.
All inputs are finite; a program needn't handle non-finite values.
Results may differ from a plain program's by a relative error of at most 0.0003.
Values sent between devices are 32-bit elements; how exact they have to be, the bound alone decides.
A program may use at most 64 MiB of HBM per device.

v0:
```python
import functools
import math

import jax
import jax.numpy as jnp
from jax import lax
from jax.experimental import pallas as pl
from jax.experimental.pallas import tpu as pltpu
from jax.sharding import PartitionSpec as P

MESH = pl.DeviceIdType.MESH
HIGHEST = lax.Precision.HIGHEST
LANES = 128


def transform_kernel(scale, tile, design_ref, signs_ref, kept_ref, out_ref, split):
    length = design_ref.shape[0]
    values = design_ref[...]
    high = values.astype(jnp.bfloat16)
    rest = values - high.astype(jnp.float32)
    middle = rest.astype(jnp.bfloat16)
    split[0] = high
    split[1] = middle
    split[2] = (rest - middle.astype(jnp.float32)).astype(jnp.bfloat16)
    first_row = lax.axis_index("rows") * length
    lane = lax.broadcasted_iota(jnp.int32, (LANES, LANES), 1)

    def step(index, carry):
        stacked = []
        for piece in range(tile // LANES):
            row = kept_ref[pl.ds(index * (tile // LANES) + piece, 1), :]
            column = jnp.broadcast_to(row, (LANES, LANES)).T
            blocks = []
            for block in range(length // LANES):
                common = jnp.bitwise_and(column, lane + (first_row + block * LANES))
                odd = jnp.bitwise_and(lax.population_count(common), 1)
                flips = signs_ref[block : block + 1, :]
                entry = (1 - 2 * odd) * flips
                blocks.append(entry.astype(jnp.float32).astype(jnp.bfloat16))
            stacked.append(jnp.concatenate(blocks, axis=1))
        table = jnp.concatenate(stacked, axis=0)
        total = jnp.dot(table, split[2], preferred_element_type=jnp.float32)
        total += jnp.dot(table, split[1], preferred_element_type=jnp.float32)
        total += jnp.dot(table, split[0], preferred_element_type=jnp.float32)
        out_ref[pl.ds(pl.multiple_of(index * tile, tile), tile), :] = total * scale
        return carry

    lax.fori_loop(0, out_ref.shape[0] // tile, step, 0)


def transform(design, signs, kept, total_rows):
    length, width = design.shape
    count = kept.shape[0]
    tile = 256
    return pl.pallas_call(
        functools.partial(transform_kernel, 1.0 / math.sqrt(total_rows), tile),
        out_shape=jax.ShapeDtypeStruct((count, width), jnp.float32),
        in_specs=[pl.BlockSpec(memory_space=pltpu.VMEM)] * 3,
        out_specs=pl.BlockSpec(memory_space=pltpu.VMEM),
        scratch_shapes=[pltpu.VMEM((3, length, width), jnp.bfloat16)],
        cost_estimate=pl.CostEstimate(
            flops=6 * count * length * width, bytes_accessed=4 * (count + length) * width, transcendentals=0
        ),
    )(design, signs.reshape(-1, LANES), kept.reshape(-1, LANES))


def exchange_kernel(
    n, orders, x_ref, sketch_ref, gram_ref, buf, recv, gat,
    rs_send, rs_recv, ag_send, ag_recv, ex_send, ex_recv,
):
    me = lax.axis_index("rows")
    core = lax.axis_index("cols")
    levels = len(orders[0])
    parts = len(orders)
    width = x_ref.shape[2]
    sub = x_ref.shape[1] // parts

    def flip(bit):
        return (1 - 2 * ((me // (1 << bit)) % 2)) * (1 << bit)

    barrier = pltpu.get_barrier_semaphore()
    for bit in range(levels):
        pl.semaphore_signal(barrier, inc=1, device_id=(me + flip(bit), core), device_id_type=MESH)
    far = flip(levels - 1) + flip(levels - 2)
    pl.semaphore_signal(barrier, inc=1, device_id=(me + far, core), device_id_type=MESH)
    pl.semaphore_signal(barrier, inc=1, device_id=(me, 1 - core), device_id_type=MESH)

    def slot_owner(part, slot):
        owner = me
        for place, bit in enumerate(orders[part]):
            if (slot >> (levels - 1 - place)) & 1:
                owner = owner + flip(bit)
        return owner

    lanes = pl.ds(pl.multiple_of(core * width, LANES), width)

    for part in range(parts):
        for slot in range(n - 1, -1, -1):
            buf[part, slot] = x_ref[slot_owner(part, slot), part * sub : (part + 1) * sub, :]
    pl.semaphore_wait(barrier, levels + 2)

    def level_of(slot):
        return levels - slot.bit_length()

    def partner(part, slot):
        return me + (far if slot == 3 else flip(orders[part][level_of(slot)]))

    def reduce_copy(part, slot):
        return pltpu.make_async_remote_copy(
            src_ref=buf.at[part, slot],
            dst_ref=recv.at[part, slot],
            send_sem=rs_send.at[part, slot],
            recv_sem=rs_recv.at[part, slot],
            device_id=(partner(part, slot), core),
            device_id_type=MESH,
        )

    for slot in range(n - 1, n // 2 - 1, -1):
        for part in range(parts):
            reduce_copy(part, slot).start()
    for slot in range(n // 2 - 1, -1, -1):
        for part in range(parts):
            total = buf[part, slot]
            terms = [slot + (1 << k) for k in range(levels - 1, -1, -1) if (1 << k) > slot]
            if slot == 1:
                terms.remove(3)
            if slot == 0:
                terms.append(3)
            for term in terms:
                reduce_copy(part, term).wait_recv()
                total += recv[part, term]
            if slot:
                buf[part, slot] = total
                reduce_copy(part, slot).start()
            else:
                sketch_ref[part * sub : (part + 1) * sub, :] = total
                gat[part, 0, :, lanes] = total

    def gather_copy(part, slot):
        source = 0 if slot == 3 else slot - (n >> (level_of(slot) + 1))
        return pltpu.make_async_remote_copy(
            src_ref=gat.at[part, source, :, lanes],
            dst_ref=gat.at[part, slot, :, lanes],
            send_sem=ag_send.at[part, slot],
            recv_sem=ag_recv.at[part, slot],
            device_id=(partner(part, slot), core),
            device_id_type=MESH,
        )

    def core_copy(part, slot):
        return pltpu.make_async_remote_copy(
            src_ref=gat.at[part, slot, :, lanes],
            dst_ref=gat.at[part, slot, :, lanes],
            send_sem=ex_send.at[part, slot],
            recv_sem=ex_recv.at[part, slot],
            device_id=(me, 1 - core),
            device_id_type=MESH,
        )

    def forward(part, slot):
        half = 1
        while half < n:
            if half > slot and slot + half != 3:
                gather_copy(part, slot + half).start()
            half *= 2
        if slot == 0:
            gather_copy(part, 3).start()
        core_copy(part, slot).start()

    def receive(slot):
        for part in range(parts):
            gather_copy(part, slot).wait_recv()
            forward(part, slot)

    def add_gram(start, size, first=False):
        whole = gat.shape[3]
        half = whole // 2
        group = min(size, 8)
        for slot in range(start, start + size):
            for part in range(parts):
                core_copy(part, slot).wait_recv()
        if first:
            gram_ref[...] = jnp.zeros_like(gram_ref)

        def step(index, carry):
            part, piece = index // (size // group), index % (size // group)
            rows = gat[part, pl.ds(start + piece * group, group)].reshape(group * sub, whole)
            dims = (((0,), (0,)), ((), ()))
            gram_ref[0:half, :] += lax.dot_general(
                rows[:, :half], rows, dims, precision=HIGHEST, preferred_element_type=jnp.float32
            )
            gram_ref[half:, half:] += lax.dot_general(
                rows[:, half:], rows[:, half:], dims, precision=HIGHEST, preferred_element_type=jnp.float32
            )
            return carry

        lax.fori_loop(0, parts * (size // group), step, 0)

    for part in range(parts):
        forward(part, 0)
    inner = sorted(range(1, n // 2), key=lambda slot: (slot.bit_count(), -slot))
    for slot in inner:
        receive(slot)
    add_gram(0, n // 2, True)
    for slot in range(n // 2, n):
        receive(slot)
    add_gram(n // 2, n // 2)
    for part in range(parts):
        for slot in range(n):
            if slot:
                reduce_copy(part, slot).wait_send()
                gather_copy(part, slot).wait_send()
            core_copy(part, slot).wait_send()


def exchange(outgoing, n, cores):
    count, width = outgoing.shape
    per = count // n
    levels = n.bit_length() - 1
    parts = 2
    orders = []
    for part in range(parts):
        order = list(range(levels))
        if part % 2 and levels > 1:
            order[0], order[1] = order[1], order[0]
        orders.append(tuple(order))
    slots = (parts, n, per // parts, width)
    sems = pltpu.SemaphoreType.DMA((parts, n))
    whole = width * cores
    return pl.pallas_call(
        functools.partial(exchange_kernel, n, tuple(orders)),
        out_shape=(
            jax.ShapeDtypeStruct((per, width), jnp.float32),
            jax.ShapeDtypeStruct((whole, whole), jnp.float32),
        ),
        in_specs=[pl.BlockSpec(memory_space=pltpu.VMEM)],
        out_specs=(pl.BlockSpec(memory_space=pltpu.VMEM),) * 2,
        scratch_shapes=[
            pltpu.VMEM(slots, jnp.float32),
            pltpu.VMEM(slots, jnp.float32),
            pltpu.VMEM((parts, n, per // parts, whole), jnp.float32),
            sems, sems, sems, sems, sems, sems,
        ],
        compiler_params=pltpu.CompilerParams(
            collective_id=0, has_side_effects=True, vmem_limit_bytes=60 * 1024 * 1024
        ),
    )(outgoing.reshape(n, per, width))


def factor_block(block, inverse):
    size = block.shape[0]
    sub = lax.broadcasted_iota(jnp.int32, (8, size), 0)
    rest_a = block
    rest_b = None
    if inverse:
        rest_b = (
            lax.broadcasted_iota(jnp.int32, (size, size), 0) == lax.broadcasted_iota(jnp.int32, (size, size), 1)
        ).astype(jnp.float32)
    upper, lower = [], []
    for group in range(size // 8):
        first = group * 8
        columns = [jnp.broadcast_to(rest_a[:, first + j : first + j + 1], rest_a.shape) for j in range(8)]
        top_c, rest_c = [c[:8] for c in columns], [c[8:] for c in columns]
        more = first + 8 < size
        top_a, rest_a = rest_a[:8], rest_a[8:]
        if inverse:
            top_b, rest_b = rest_b[:8], rest_b[8:]
        for j in range(8):
            root = lax.rsqrt(top_c[j][j : j + 1])
            top_s = jnp.where(sub > j, top_c[j] * root, 0.0)
            row_a = top_a[j : j + 1] * root
            top_a = jnp.where(sub == j, row_a, top_a - top_s * row_a)
            if more:
                rest_s = rest_c[j] * root
                rest_a = rest_a - rest_s * row_a
            if inverse:
                row_b = top_b[j : j + 1] * root
                top_b = jnp.where(sub == j, row_b, top_b - top_s * row_b)
                if more:
                    rest_b = rest_b - rest_s * row_b
            for later in range(j + 1, 8):
                weight = top_c[later][j : j + 1] * root
                top_c[later] = top_c[later] - top_s * weight
                if more:
                    rest_c[later] = rest_c[later] - rest_s * weight
        upper.append(top_a)
        if inverse:
            lower.append(top_b)
    return jnp.concatenate(upper, axis=0), (jnp.concatenate(lower, axis=0) if inverse else None)


def cholesky_kernel(scale, gram_ref, out_ref, work, upper):
    size = gram_ref.shape[0]
    block = LANES
    work[...] = gram_ref[...] * scale
    upper[...] = jnp.zeros_like(upper)
    triangle = lax.broadcasted_iota(jnp.int32, (block, block), 0) <= lax.broadcasted_iota(
        jnp.int32, (block, block), 1
    )
    dims = (((0,), (0,)), ((), ()))
    for start in range(0, size, block):
        stop = start + block
        last = stop == size
        diagonal, inverse = factor_block(work[start:stop, start:stop], not last)
        upper[start:stop, start:stop] = jnp.where(triangle, diagonal, 0.0)
        if not last:
            panel = jnp.dot(
                inverse, work[start:stop, stop:], precision=HIGHEST, preferred_element_type=jnp.float32
            )
            upper[start:stop, stop:] = panel
            for row in range(stop, size, block):
                work[row : row + block, row:] -= lax.dot_general(
                    panel[:, row - stop : row - stop + block],
                    panel[:, row - stop :],
                    dims,
                    precision=HIGHEST,
                    preferred_element_type=jnp.float32,
                )
    width = out_ref.shape[1]
    out_ref[...] = upper[:, pl.ds(pl.multiple_of(lax.axis_index("cols") * width, width), width)]


def cholesky(gram, scale, width):
    size = gram.shape[0]
    return pl.pallas_call(
        functools.partial(cholesky_kernel, scale),
        out_shape=jax.ShapeDtypeStruct((size, width), jnp.float32),
        in_specs=[pl.BlockSpec(memory_space=pltpu.VMEM)],
        out_specs=pl.BlockSpec(memory_space=pltpu.VMEM),
        scratch_shapes=[pltpu.VMEM((size, size), jnp.float32)] * 2,
    )(gram)


def solution(mesh):
    n, cores = mesh.shape["rows"], mesh.shape["cols"]

    def body(design, signs, kept):
        widths = design.shape[1]
        outgoing = transform(design, signs, kept, design.shape[0] * n)
        sketch, gram = exchange(outgoing, n, cores)
        return (sketch, cholesky(gram, 1.0 / kept.shape[0], widths))

    return jax.shard_map(
        body,
        mesh=mesh,
        in_specs=(P("rows", "cols"), P("rows"), P()),
        out_specs=(P("rows", "cols"), P(None, "cols")),
        check_vma=False,
    )
```

profile of v0, /device:TPU:0, one launch (start us, length us, event | category | flops | bytes accessed | tf_op | source)
XLA Modules:
  0.0 68.9 jit_solution(16898648272741580391)
XLA Ops:
  0.6 5.4 %shard_map.50 = f32[1024,256]{1,0:T(8,128)} custom-call(f32[1024,256]{1,0:T(8,128)} %design_ref.1, s32[8,128]{1,0:T(8,128)} %bitcast.4, s32[8,128]{1,0:T(8,128)} %bitcast.5), custom_call_target="tpu_custom_call" | custom-call | flops 1610612736 | bytes 2097152 | tf_op jit(solution)/shard_map/pallas_call | solution.py:55
  6.0 43.5 %shard_map.51 = (f32[64,256]{1,0:T(8,128)}, f32[512,512]{1,0:T(8,128)}) custom-call(f32[16,64,256]{2,1,0:T(8,128)} %bitcast.3), custom_call_target="tpu_custom_call" | custom-call | tf_op jit(solution)/shard_map/pallas_call | solution.py:230
  49.5 0.0 copy-start
  49.5 18.8 %shard_map.52 = f32[512,256]{1,0:T(8,128)} custom-call(f32[512,512]{1,0:T(8,128)} %get-tuple-element.5.gram_ref), custom_call_target="tpu_custom_call" | custom-call | tf_op jit(solution)/shard_map/pallas_call | solution.py:325
  68.3 0.0 copy-done
  68.3 0.6 copy.6
Async XLA Ops:
  49.5 18.8 %copy-start = (f32[64,256]{1,0:T(8,128)S(1)}, f32[64,256]{1,0:T(8,128)}, u32[]{:S(2)}) copy-start(f32[64,256]{1,0:T(8,128)} %get-tuple-element.8) | copy-start | bytes 196612
where the time goes:
time: 69.1 us; the launch traced here: 68.9 us
  Pallas kernels  67.6 us (98%)
    pallas_call x1, Pallas kernels, exchange(): pl.pallas_call(functools.partial(exchange_kernel, n, tuple(orders)), out_...  43.5 us
    pallas_call x1, Pallas kernels, cholesky(): pl.pallas_call(functools.partial(cholesky_kernel, scale), out_shape=jax.S...  18.8 us
    pallas_call x1, Pallas kernels, transform(): pl.pallas_call(functools.partial(transform_kernel, 1.0 / math.sqrt(total_...  5.37 us

commit v1 on v0

--- a/solution.py
+++ b/solution.py
@@ -17,11 +17,8 @@
     length = design_ref.shape[0]
     values = design_ref[...]
     high = values.astype(jnp.bfloat16)
-    rest = values - high.astype(jnp.float32)
-    middle = rest.astype(jnp.bfloat16)
     split[0] = high
-    split[1] = middle
-    split[2] = (rest - middle.astype(jnp.float32)).astype(jnp.bfloat16)
+    split[1] = (values - high.astype(jnp.float32)).astype(jnp.bfloat16)
     first_row = lax.axis_index("rows") * length
     lane = lax.broadcasted_iota(jnp.int32, (LANES, LANES), 1)
 
@@ -39,8 +36,7 @@
                 blocks.append(entry.astype(jnp.float32).astype(jnp.bfloat16))
             stacked.append(jnp.concatenate(blocks, axis=1))
         table = jnp.concatenate(stacked, axis=0)
-        total = jnp.dot(table, split[2], preferred_element_type=jnp.float32)
-        total += jnp.dot(table, split[1], preferred_element_type=jnp.float32)
+        total = jnp.dot(table, split[1], preferred_element_type=jnp.float32)
         total += jnp.dot(table, split[0], preferred_element_type=jnp.float32)
         out_ref[pl.ds(pl.multiple_of(index * tile, tile), tile), :] = total * scale
         return carry
@@ -57,9 +53,9 @@
         out_shape=jax.ShapeDtypeStruct((count, width), jnp.float32),
         in_specs=[pl.BlockSpec(memory_space=pltpu.VMEM)] * 3,
         out_specs=pl.BlockSpec(memory_space=pltpu.VMEM),
-        scratch_shapes=[pltpu.VMEM((3, length, width), jnp.bfloat16)],
+        scratch_shapes=[pltpu.VMEM((2, length, width), jnp.bfloat16)],
         cost_estimate=pl.CostEstimate(
-            flops=6 * count * length * width, bytes_accessed=4 * (count + length) * width, transcendentals=0
+            flops=4 * count * length * width, bytes_accessed=4 * (count + length) * width, transcendentals=0
         ),
     )(design, signs.reshape(-1, LANES), kept.reshape(-1, LANES))
 
@@ -186,11 +182,14 @@
             part, piece = index // (size // group), index % (size // group)
             rows = gat[part, pl.ds(start + piece * group, group)].reshape(group * sub, whole)
             dims = (((0,), (0,)), ((), ()))
+            high, low = split3(rows)
+            left = jnp.concatenate([high, high, low], axis=0)
+            right = jnp.concatenate([high, low, high], axis=0)
             gram_ref[0:half, :] += lax.dot_general(
-                rows[:, :half], rows, dims, precision=HIGHEST, preferred_element_type=jnp.float32
+                left[:, :half], right, dims, preferred_element_type=jnp.float32
             )
             gram_ref[half:, half:] += lax.dot_general(
-                rows[:, half:], rows[:, half:], dims, precision=HIGHEST, preferred_element_type=jnp.float32
+                left[:, half:], right[:, half:], dims, preferred_element_type=jnp.float32
             )
             return carry
 
@@ -247,83 +246,81 @@
     )(outgoing.reshape(n, per, width))
 
 
-def factor_block(block, inverse):
-    size = block.shape[0]
-    sub = lax.broadcasted_iota(jnp.int32, (8, size), 0)
-    rest_a = block
-    rest_b = None
-    if inverse:
-        rest_b = (
-            lax.broadcasted_iota(jnp.int32, (size, size), 0) == lax.broadcasted_iota(jnp.int32, (size, size), 1)
-        ).astype(jnp.float32)
-    upper, lower = [], []
-    for group in range(size // 8):
-        first = group * 8
-        columns = [jnp.broadcast_to(rest_a[:, first + j : first + j + 1], rest_a.shape) for j in range(8)]
-        top_c, rest_c = [c[:8] for c in columns], [c[8:] for c in columns]
-        more = first + 8 < size
-        top_a, rest_a = rest_a[:8], rest_a[8:]
-        if inverse:
-            top_b, rest_b = rest_b[:8], rest_b[8:]
+def spread(x, lane):
+    return jnp.broadcast_to(x[:, lane:lane+1], x.shape)
+
+def factor_panel(rows, first):
+    depth = len(rows)
+    tiles = len(rows[0])
+    sub = lax.broadcasted_iota(jnp.int32, (8, LANES), 0)
+    rows = [list(r) for r in rows]
+    ahead = [[spread(rows[r][0], first + j) for r in range(depth)] for j in range(8)]
+    done = []
+    for g in range(depth):
+        here = ahead
+        if g + 1 < depth:
+            ahead = [[spread(rows[r][0], first + 8 * (g + 1) + j) for r in range(g + 1, depth)] for j in range(8)]
+        top = rows[g]
         for j in range(8):
-            root = lax.rsqrt(top_c[j][j : j + 1])
-            top_s = jnp.where(sub > j, top_c[j] * root, 0.0)
-            row_a = top_a[j : j + 1] * root
-            top_a = jnp.where(sub == j, row_a, top_a - top_s * row_a)
-            if more:
-                rest_s = rest_c[j] * root
-                rest_a = rest_a - rest_s * row_a
-            if inverse:
-                row_b = top_b[j : j + 1] * root
-                top_b = jnp.where(sub == j, row_b, top_b - top_s * row_b)
-                if more:
-                    rest_b = rest_b - rest_s * row_b
+            column = here[j]
+            root = lax.rsqrt(column[0][j:j+1])
+            root = jnp.broadcast_to(root, (8, LANES))
+            scaled = [c * root for c in column]
             for later in range(j + 1, 8):
-                weight = top_c[later][j : j + 1] * root
-                top_c[later] = top_c[later] - top_s * weight
-                if more:
-                    rest_c[later] = rest_c[later] - rest_s * weight
-        upper.append(top_a)
-        if inverse:
-            lower.append(top_b)
-    return jnp.concatenate(upper, axis=0), (jnp.concatenate(lower, axis=0) if inverse else None)
-
-
-def cholesky_kernel(scale, gram_ref, out_ref, work, upper):
+                weight = here[later][0][j:j+1] * root
+                here[later] = [c - s * weight for c, s in zip(here[later], scaled)]
+            below = jnp.where(sub > j, scaled[0], 0.0)
+            lines = [t[j:j+1] * root for t in top]
+            top = [jnp.where(sub == j, l, t - below * l) for t, l in zip(top, lines)]
+            for r in range(g + 1, depth):
+                rows[r] = [x - scaled[r - g] * l for x, l in zip(rows[r], lines)]
+            if g + 1 < depth:
+                for l in range(8):
+                    weight = scaled[1][l:l+1]
+                    ahead[l] = [c - s * weight for c, s in zip(ahead[l], scaled[1:])]
+        done.append(top)
+    return done
+
+def split3(x):
+    high = x.astype(jnp.bfloat16)
+    low = (x - high.astype(jnp.float32)).astype(jnp.bfloat16)
+    return high, low
+
+def cholesky_kernel(scale, panel, gram_ref, out_ref, work, upper):
     size = gram_ref.shape[0]
-    block = LANES
+    tiles = size // LANES
+    depth = panel // 8
     work[...] = gram_ref[...] * scale
     upper[...] = jnp.zeros_like(upper)
-    triangle = lax.broadcasted_iota(jnp.int32, (block, block), 0) <= lax.broadcasted_iota(
-        jnp.int32, (block, block), 1
-    )
     dims = (((0,), (0,)), ((), ()))
-    for start in range(0, size, block):
-        stop = start + block
-        last = stop == size
-        diagonal, inverse = factor_block(work[start:stop, start:stop], not last)
-        upper[start:stop, start:stop] = jnp.where(triangle, diagonal, 0.0)
-        if not last:
-            panel = jnp.dot(
-                inverse, work[start:stop, stop:], precision=HIGHEST, preferred_element_type=jnp.float32
-            )
-            upper[start:stop, stop:] = panel
-            for row in range(stop, size, block):
-                work[row : row + block, row:] -= lax.dot_general(
-                    panel[:, row - stop : row - stop + block],
-                    panel[:, row - stop :],
-                    dims,
-                    precision=HIGHEST,
-                    preferred_element_type=jnp.float32,
-                )
+    for start in range(0, size, panel):
+        t0 = start // LANES
+        first = start - t0 * LANES
+        rows = [[work[start + 8*r : start + 8*r + 8, t*LANES:(t+1)*LANES] for t in range(t0, tiles)] for r in range(depth)]
+        done = factor_panel(rows, first)
+        full = jnp.concatenate([jnp.concatenate(d, axis=1) for d in done], axis=0)
+        row = lax.broadcasted_iota(jnp.int32, full.shape, 0) + first
+        col = lax.broadcasted_iota(jnp.int32, full.shape, 1)
+        full = jnp.where(row <= col, full, 0.0)
+        upper[start:start+panel, t0*LANES:] = full
+        stop = start + panel
+        if stop == size: break
+        high, low = split3(full)
+        left = jnp.concatenate([high, high, low], axis=0)
+        right = jnp.concatenate([high, low, high], axis=0)
+        for t in range(stop // LANES, tiles):
+            lo = max(stop, t * LANES)
+            off = (t - t0) * LANES
+            prod = lax.dot_general(left[:, off:off+LANES], right[:, off:], dims, preferred_element_type=jnp.float32)
+            work[lo:(t+1)*LANES, t*LANES:] -= prod[lo - t*LANES:]
     width = out_ref.shape[1]
-    out_ref[...] = upper[:, pl.ds(pl.multiple_of(lax.axis_index("cols") * width, width), width)]
-
-
-def cholesky(gram, scale, width):
+    if width == size: out_ref[...] = upper[...]
+    else: out_ref[...] = upper[:, pl.ds(pl.multiple_of(lax.axis_index("cols") * width, width), width)]
+
+def cholesky(gram, scale, width, panel=32):
     size = gram.shape[0]
     return pl.pallas_call(
-        functools.partial(cholesky_kernel, scale),
+        functools.partial(cholesky_kernel, scale, panel),
         out_shape=jax.ShapeDtypeStruct((size, width), jnp.float32),
         in_specs=[pl.BlockSpec(memory_space=pltpu.VMEM)],
         out_specs=pl.BlockSpec(memory_space=pltpu.VMEM),

time: 69.1 us -> 61.5 us (0.89)
  Pallas kernels: 67.6 us -> 60 us
    pallas_call x1, Pallas kernels: 18.8 us -> 13.3 us  [cholesky(): pl.pallas_call(functools.partial(cholesky_kernel, scale, panel), out_shap...]
    pallas_call x1, Pallas kernels: 43.5 us -> 42.3 us  [exchange(): pl.pallas_call(functools.partial(exchange_kernel, n, tuple(orders)), out_...]
    pallas_call x1, Pallas kernels: 5.37 us -> 4.38 us  [transform(): pl.pallas_call(functools.partial(transform_kernel, 1.0 / math.sqrt(total_...]
where the time goes in v1:
time: 61.5 us; the launch traced here: 61.3 us
  Pallas kernels  60 us (98%)
  between operations  0.65 us (1%)
  local copies, waits for them, and re-layouts  0.63 us (1%)
    pallas_call x1, Pallas kernels, exchange(): pl.pallas_call(functools.partial(exchange_kernel, n, tuple(orders)), out_...  42.3 us
    pallas_call x1, Pallas kernels, cholesky(): pl.pallas_call(functools.partial(cholesky_kernel, scale, panel), out_shap...  13.3 us
    pallas_call x1, Pallas kernels, transform(): pl.pallas_call(functools.partial(transform_kernel, 1.0 / math.sqrt(total_...  4.38 us

profile of v1, /device:TPU:0, one launch (start us, length us, event | category | flops | bytes accessed | tf_op | source)
XLA Modules:
  0.0 61.3 jit_solution(2559051008067277596)
XLA Ops:
  0.6 4.4 %shard_map.50 = f32[1024,256]{1,0:T(8,128)} custom-call(f32[1024,256]{1,0:T(8,128)} %design_ref.1, s32[8,128]{1,0:T(8,128)} %bitcast.4, s32[8,128]{1,0:T(8,128)} %bitcast.5), custom_call_target="tpu_custom_call" | custom-call | flops 1073741824 | bytes 2097152 | tf_op jit(solution)/shard_map/pallas_call | solution.py:51
  5.0 42.3 %shard_map.51 = (f32[64,256]{1,0:T(8,128)}, f32[512,512]{1,0:T(8,128)}) custom-call(f32[16,64,256]{2,1,0:T(8,128)} %bitcast.3), custom_call_target="tpu_custom_call" | custom-call | tf_op jit(solution)/shard_map/pallas_call | solution.py:229
  47.4 0.0 copy-start
  47.4 13.3 %shard_map.52 = f32[512,256]{1,0:T(8,128)} custom-call(f32[512,512]{1,0:T(8,128)} %get-tuple-element.5.gram_ref), custom_call_target="tpu_custom_call" | custom-call | tf_op jit(solution)/shard_map/pallas_call | solution.py:322
  60.7 0.0 copy-done
  60.7 0.6 %copy.6 = f32[64,256]{1,0:T(8,128)} copy(f32[64,256]{1,0:T(8,128)S(1)} %copy-done) | data formatting | bytes 131072
Async XLA Ops:
  47.4 13.3 %copy-start = (f32[64,256]{1,0:T(8,128)S(1)}, f32[64,256]{1,0:T(8,128)}, u32[]{:S(2)}) copy-start(f32[64,256]{1,0:T(8,128)} %get-tuple-element.8) | copy-start | bytes 196612

commit v2 on v1

v2 whole, which is shorter than its diff:
```python
import functools
import math

import jax
import jax.numpy as jnp
from jax import lax
from jax.experimental import pallas as pl
from jax.experimental.pallas import tpu as pltpu
from jax.sharding import PartitionSpec as P

MESH = pl.DeviceIdType.MESH
LANES = 128


def split_two(values):
    high = values.astype(jnp.bfloat16)
    return high, (values - high.astype(jnp.float32)).astype(jnp.bfloat16)


def sketch_kernel(
    low, scale, early,
    design_ref, signs_ref, kept_ref, sketch_ref, gram_ref,
    split, buf, one_a, one_b, out_a, out_b, two_a, two_b, gat,
    one_a_send, one_a_recv, one_b_send, one_b_recv, two_a_send, two_a_recv, two_b_send, two_b_recv,
    az_send, az_recv, axy_send, axy_recv, bxy_send, bxy_recv, bz_send, bz_recv,
    ca_send, ca_recv, cb_send, cb_recv,
):
    me = lax.axis_index("rows")
    core = lax.axis_index("cols")
    high, _, per, width = buf.shape
    length = design_ref.shape[0]
    tile = low * per
    whole = gat.shape[2]
    spot = me % low
    lanes = pl.ds(pl.multiple_of(core * width, LANES), width)
    head, tail = pl.ds(0, early), pl.ds(early, per - early)

    def flip(value, mask):
        bit = 1
        while bit <= mask:
            if mask & bit:
                value = value + (1 - 2 * ((value // bit) % 2)) * bit
            bit *= 2
        return value

    def peer(near, far):
        return flip(me, far * low + near)

    def plane(far):
        return flip(me // low, far)

    def send(src, dst, sems, index, device, other=None):
        return pltpu.make_async_remote_copy(
            src_ref=src, dst_ref=dst, send_sem=sems[0].at[index], recv_sem=sems[1].at[index],
            device_id=(device, core if other is None else other), device_id_type=MESH,
        )

    nears = list(range(low - 1, 0, -1))
    fars = list(range(high - 1, 0, -1))

    barrier = pltpu.get_barrier_semaphore()
    for near in nears:
        pl.semaphore_signal(barrier, inc=1, device_id=(peer(near, 0), core), device_id_type=MESH)
    for far in fars:
        pl.semaphore_signal(barrier, inc=1, device_id=(peer(0, far), core), device_id_type=MESH)
    pl.semaphore_signal(barrier, inc=1, device_id=(me, 1 - core), device_id_type=MESH)

    def one_a_copy(far, near):
        return send(
            buf.at[far, flip(spot, near), head], one_a.at[far, near], (one_a_send, one_a_recv), (far, near),
            peer(near, 0),
        )

    def one_b_copy(far):
        return send(buf.at[far, :, tail], one_b.at[far], (one_b_send, one_b_recv), far, peer(0, far))

    def two_a_copy(far):
        return send(out_a.at[far], two_a.at[far], (two_a_send, two_a_recv), far, peer(0, far))

    def two_b_copy(near):
        return send(
            out_b.at[flip(spot, near)], two_b.at[near], (two_b_send, two_b_recv), near, peer(near, 0)
        )

    def az_copy(far):
        ref = gat.at[me, head, lanes]
        return send(ref, ref, (az_send, az_recv), far, peer(0, far))

    def axy_copy(far, near):
        ref = gat.at[peer(0, far), head, lanes]
        return send(ref, ref, (axy_send, axy_recv), (far, near), peer(near, 0))

    def bxy_copy(near):
        ref = gat.at[me, tail, lanes]
        return send(ref, ref, (bxy_send, bxy_recv), near, peer(near, 0))

    def bz_copy(far):
        ref = gat.at[pl.ds((me // low) * low, low), tail, lanes]
        return send(ref, ref, (bz_send, bz_recv), far, peer(0, far))

    def ca_copy(far, near):
        ref = gat.at[peer(near, far), head, lanes]
        return send(ref, ref, (ca_send, ca_recv), (far, near), me, 1 - core)

    def cb_copy(far):
        ref = gat.at[pl.ds(plane(far) * low, low), tail, lanes]
        return send(ref, ref, (cb_send, cb_recv), far, me, 1 - core)

    split[0], split[1] = split_two(design_ref[...])
    first_row = me * length
    lane = lax.broadcasted_iota(jnp.int32, (LANES, LANES), 1)
    step_rows = min(tile, 256)

    def transform_rows(far, start):
        stacked = []
        for piece in range(step_rows // LANES):
            row = kept_ref[pl.ds(plane(far) * (tile // LANES) + start // LANES + piece, 1), :]
            column = jnp.broadcast_to(row, (LANES, LANES)).T
            blocks = []
            for block in range(length // LANES):
                common = jnp.bitwise_and(column, lane + (first_row + block * LANES))
                odd = jnp.bitwise_and(lax.population_count(common), 1)
                flips = signs_ref[block : block + 1, :]
                entry = (1 - 2 * odd) * flips
                blocks.append(entry.astype(jnp.float32).astype(jnp.bfloat16))
            stacked.append(jnp.concatenate(blocks, axis=1))
        table = jnp.concatenate(stacked, axis=0)
        total = jnp.dot(table, split[1], preferred_element_type=jnp.float32)
        total += jnp.dot(table, split[0], preferred_element_type=jnp.float32)
        owner = start // per
        buf[far, owner : owner + step_rows // per] = (total * scale).reshape(step_rows // per, per, width)

    for far in fars + [0]:
        for start in range(0, tile, step_rows):
            transform_rows(far, start)
        if far == high - 1:
            pl.semaphore_wait(barrier, len(nears) + len(fars) + 1)
        for near in nears:
            one_a_copy(far, near).start()
        if far:
            one_b_copy(far).start()

    def near_sum(far):
        total = buf[far, spot, head]
        for near in nears:
            one_a_copy(far, near).wait_recv()
            total += one_a[far, near]
        return total

    for far in fars:
        out_a[far] = near_sum(far)
        two_a_copy(far).start()
    total = buf[0, :, tail]
    for far in fars:
        one_b_copy(far).wait_recv()
        total += one_b[far]
    out_b[...] = total
    for near in nears:
        two_b_copy(near).start()
    total = near_sum(0)
    for far in fars:
        two_a_copy(far).wait_recv()
        total += two_a[far]
    sketch_ref[head, :] = total
    gat[me, head, lanes] = total
    for far in fars:
        az_copy(far).start()
    for near in nears:
        axy_copy(0, near).start()
    ca_copy(0, 0).start()
    total = out_b[spot]
    for near in nears:
        two_b_copy(near).wait_recv()
        total += two_b[near]
    sketch_ref[tail, :] = total
    gat[me, tail, lanes] = total
    for near in nears:
        bxy_copy(near).start()

    def add_gram(far, first):
        for near in range(low):
            ca_copy(far, near).wait_recv()
        cb_copy(far).wait_recv()
        half = whole // 2
        rows = gat[pl.ds(plane(far) * low, low)].reshape(tile, whole)
        upper, rest = split_two(rows)
        left = jnp.concatenate([upper, upper, rest], axis=0)
        right = jnp.concatenate([upper, rest, upper], axis=0)
        dims = (((0,), (0,)), ((), ()))
        a = lax.dot_general(left[:, :half], right, dims, preferred_element_type=jnp.float32)
        c = lax.dot_general(left[:, half:], right[:, half:], dims, preferred_element_type=jnp.float32)
        gram_ref[0:half, :] = a if first else gram_ref[0:half, :] + a
        gram_ref[half:, half:] = c if first else gram_ref[half:, half:] + c

    for near in nears:
        bxy_copy(near).wait_recv()
    for far in fars:
        bz_copy(far).start()
    cb_copy(0).start()
    for near in nears:
        axy_copy(0, near).wait_recv()
        ca_copy(0, near).start()
    for far in fars:
        az_copy(far).wait_recv()
        for near in nears:
            axy_copy(far, near).start()
        ca_copy(far, 0).start()
    gram_ref[half_rows(gram_ref) :, : whole // 2] = jnp.zeros((whole // 2, whole // 2), jnp.float32)
    add_gram(0, True)
    for far in fars:
        for near in nears:
            axy_copy(far, near).wait_recv()
            ca_copy(far, near).start()
        bz_copy(far).wait_recv()
        cb_copy(far).start()
        add_gram(far, False)

    for far in range(high):
        for near in range(low):
            if near:
                one_a_copy(far, near).wait_send()
                axy_copy(far, near).wait_send()
            ca_copy(far, near).wait_send()
        cb_copy(far).wait_send()
        if far:
            one_b_copy(far).wait_send()
            two_a_copy(far).wait_send()
            az_copy(far).wait_send()
            bz_copy(far).wait_send()
    for near in nears:
        two_b_copy(near).wait_send()
        bxy_copy(near).wait_send()


def half_rows(ref):
    return ref.shape[0] // 2


def sketch_and_gram(design, signs, kept, n, cores):
    length, width = design.shape
    count = kept.shape[0]
    per = count // n
    low = 1 << ((n.bit_length() - 1) // 2)
    high = n // low
    early = per - per // 4
    whole = width * cores
    sems = []
    for shape in ((high, low), (high,), (high,), (low,), (high,), (high, low), (low,), (high,), (high, low), (high,)):
        sems += [pltpu.SemaphoreType.DMA(shape)] * 2
    late = per - early
    return pl.pallas_call(
        functools.partial(sketch_kernel, low, 1.0 / math.sqrt(length * n), early),
        out_shape=(
            jax.ShapeDtypeStruct((per, width), jnp.float32),
            jax.ShapeDtypeStruct((whole, whole), jnp.float32),
        ),
        in_specs=[pl.BlockSpec(memory_space=pltpu.VMEM)] * 3,
        out_specs=(pl.BlockSpec(memory_space=pltpu.VMEM),) * 2,
        scratch_shapes=[
            pltpu.VMEM((2, length, width), jnp.bfloat16),
            pltpu.VMEM((high, low, per, width), jnp.float32),
            pltpu.VMEM((high, low, early, width), jnp.float32),
            pltpu.VMEM((high, low, late, width), jnp.float32),
            pltpu.VMEM((high, early, width), jnp.float32),
            pltpu.VMEM((low, late, width), jnp.float32),
            pltpu.VMEM((high, early, width), jnp.float32),
            pltpu.VMEM((low, late, width), jnp.float32),
            pltpu.VMEM((n, per, whole), jnp.float32),
            *sems,
        ],
        compiler_params=pltpu.CompilerParams(
            collective_id=0, has_side_effects=True, vmem_limit_bytes=60 * 1024 * 1024
        ),
    )(design, signs.reshape(-1, LANES), kept.reshape(-1, LANES))


def spread(x, lane):
    return jnp.broadcast_to(x[:, lane:lane+1], x.shape)

def factor_panel(rows, first):
    depth = len(rows)
    tiles = len(rows[0])
    sub = lax.broadcasted_iota(jnp.int32, (8, LANES), 0)
    rows = [list(r) for r in rows]
    ahead = [[spread(rows[r][0], first + j) for r in range(depth)] for j in range(8)]
    done = []
    for g in range(depth):
        here = ahead
        if g + 1 < depth:
            ahead = [[spread(rows[r][0], first + 8 * (g + 1) + j) for r in range(g + 1, depth)] for j in range(8)]
        top = rows[g]
        for j in range(8):
            column = here[j]
            root = lax.rsqrt(column[0][j:j+1])
            root = jnp.broadcast_to(root, (8, LANES))
            scaled = [c * root for c in column]
            for later in range(j + 1, 8):
                weight = here[later][0][j:j+1] * root
                here[later] = [c - s * weight for c, s in zip(here[later], scaled)]
            below = jnp.where(sub > j, scaled[0], 0.0)
            lines = [t[j:j+1] * root for t in top]
            top = [jnp.where(sub == j, l, t - below * l) for t, l in zip(top, lines)]
            for r in range(g + 1, depth):
                rows[r] = [x - scaled[r - g] * l for x, l in zip(rows[r], lines)]
            if g + 1 < depth:
                for l in range(8):
                    weight = scaled[1][l:l+1]
                    ahead[l] = [c - s * weight for c, s in zip(ahead[l], scaled[1:])]
        done.append(top)
    return done

def cholesky_kernel(scale, panel, gram_ref, out_ref, work, upper):
    size = gram_ref.shape[0]
    tiles = size // LANES
    depth = panel // 8
    work[...] = gram_ref[...] * scale
    upper[...] = jnp.zeros_like(upper)
    dims = (((0,), (0,)), ((), ()))
    for start in range(0, size, panel):
        t0 = start // LANES
        first = start - t0 * LANES
        rows = [[work[start + 8*r : start + 8*r + 8, t*LANES:(t+1)*LANES] for t in range(t0, tiles)] for r in range(depth)]
        done = factor_panel(rows, first)
        full = jnp.concatenate([jnp.concatenate(d, axis=1) for d in done], axis=0)
        row = lax.broadcasted_iota(jnp.int32, full.shape, 0) + first
        col = lax.broadcasted_iota(jnp.int32, full.shape, 1)
        full = jnp.where(row <= col, full, 0.0)
        upper[start:start+panel, t0*LANES:] = full
        stop = start + panel
        if stop == size: break
        high, low = split_two(full)
        left = jnp.concatenate([high, high, low], axis=0)
        right = jnp.concatenate([high, low, high], axis=0)
        for t in range(stop // LANES, tiles):
            lo = max(stop, t * LANES)
            off = (t - t0) * LANES
            prod = lax.dot_general(left[:, off:off+LANES], right[:, off:], dims, preferred_element_type=jnp.float32)
            work[lo:(t+1)*LANES, t*LANES:] -= prod[lo - t*LANES:]
    width = out_ref.shape[1]
    if width == size: out_ref[...] = upper[...]
    else: out_ref[...] = upper[:, pl.ds(pl.multiple_of(lax.axis_index("cols") * width, width), width)]

def cholesky(gram, scale, width, panel=32):
    size = gram.shape[0]
    return pl.pallas_call(
        functools.partial(cholesky_kernel, scale, panel),
        out_shape=jax.ShapeDtypeStruct((size, width), jnp.float32),
        in_specs=[pl.BlockSpec(memory_space=pltpu.VMEM)],
        out_specs=pl.BlockSpec(memory_space=pltpu.VMEM),
        scratch_shapes=[pltpu.VMEM((size, size), jnp.float32)] * 2,
    )(gram)


def solution(mesh):
    n, cores = mesh.shape["rows"], mesh.shape["cols"]

    def body(design, signs, kept):
        sketch, gram = sketch_and_gram(design, signs, kept, n, cores)
        return (sketch, cholesky(gram, 1.0 / kept.shape[0], design.shape[1]))

    return jax.shard_map(
        body,
        mesh=mesh,
        in_specs=(P("rows", "cols"), P("rows"), P()),
        out_specs=(P("rows", "cols"), P(None, "cols")),
        check_vma=False,
    )
```

time: 61.5 us -> 52 us (0.85)
  Pallas kernels: 60 us -> 49.9 us
    pallas_call x2 -> x1, Pallas kernels: 46.7 us -> 36.6 us  [sketch_and_gram(): pl.pallas_call(functools.partial(sketch_kernel, low, 1.0 / math.sqrt(leng...]
where the time goes in v2:
time: 52 us; the launch traced here: 51.2 us
  Pallas kernels  49.9 us (96%)
  between operations  0.65 us (1%)
  local copies, waits for them, and re-layouts  0.63 us (1%)
    pallas_call x1, Pallas kernels, sketch_and_gram(): pl.pallas_call(functools.partial(sketch_kernel, low, 1.0 / math.sqrt(leng...  36.6 us
    pallas_call x1, Pallas kernels, cholesky(): pl.pallas_call(functools.partial(cholesky_kernel, scale, panel), out_shap...  13.3 us

profile of v2, /device:TPU:0, one launch (start us, length us, event | category | flops | bytes accessed | tf_op | source)
XLA Modules:
  0.0 51.2 jit_solution(10735744542710487501)
XLA Ops:
  0.6 36.6 %shard_map.50 = (f32[64,256]{1,0:T(8,128)}, f32[512,512]{1,0:T(8,128)}) custom-call(f32[1024,256]{1,0:T(8,128)} %design_ref.1, s32[8,128]{1,0:T(8,128)} %bitcast.2, s32[8,128]{1,0:T(8,128)} %bitcast.3), custom_call_target="tpu_custom_call" | custom-call | tf_op jit(solution)/shard_map/pallas_call | solution.py:251
  37.2 0.0 copy-start
  37.3 13.3 %shard_map.51 = f32[512,256]{1,0:T(8,128)} custom-call(f32[512,512]{1,0:T(8,128)} %get-tuple-element.5.gram_ref), custom_call_target="tpu_custom_call" | custom-call | tf_op jit(solution)/shard_map/pallas_call | solution.py:345
  50.6 0.0 copy-done
  50.6 0.6 %copy.6 = f32[64,256]{1,0:T(8,128)} copy(f32[64,256]{1,0:T(8,128)S(1)} %copy-done) | data formatting | bytes 131072
Async XLA Ops:
  37.2 13.3 %copy-start = (f32[64,256]{1,0:T(8,128)S(1)}, f32[64,256]{1,0:T(8,128)}, u32[]{:S(2)}) copy-start(f32[64,256]{1,0:T(8,128)} %get-tuple-element.8) | copy-start | bytes 196612

commit v3 on v2

--- a/solution.py
+++ b/solution.py
@@ -10,6 +10,7 @@
 
 MESH = pl.DeviceIdType.MESH
 LANES = 128
+LOADS = 2
 
 
 def split_two(values):
@@ -19,8 +20,8 @@
 
 def sketch_kernel(
     low, scale, early,
-    design_ref, signs_ref, kept_ref, sketch_ref, gram_ref,
-    split, buf, one_a, one_b, out_a, out_b, two_a, two_b, gat,
+    design_hbm, signs_hbm, kept_hbm, sketch_ref, gram_ref,
+    design_ref, signs_ref, kept_ref, load_sems, split, buf, one_a, one_b, out_a, out_b, two_a, two_b, gat,
     one_a_send, one_a_recv, one_b_send, one_b_recv, two_a_send, two_a_recv, two_b_send, two_b_recv,
     az_send, az_recv, axy_send, axy_recv, bxy_send, bxy_recv, bz_send, bz_recv,
     ca_send, ca_recv, cb_send, cb_recv,
@@ -28,6 +29,18 @@
     me = lax.axis_index("rows")
     core = lax.axis_index("cols")
     high, _, per, width = buf.shape
+    loads = [
+        pltpu.make_async_copy(kept_hbm, kept_ref, load_sems.at[0]),
+        pltpu.make_async_copy(signs_hbm, signs_ref, load_sems.at[1]),
+    ]
+    chunk = design_ref.shape[0] // LOADS
+    for index in range(LOADS):
+        piece = pl.ds(index * chunk, chunk)
+        loads.append(
+            pltpu.make_async_copy(design_hbm.at[piece], design_ref.at[piece], load_sems.at[2 + index])
+        )
+    for load in loads:
+        load.start()
     length = design_ref.shape[0]
     tile = low * per
     whole = gat.shape[2]
@@ -106,7 +119,6 @@
         ref = gat.at[pl.ds(plane(far) * low, low), tail, lanes]
         return send(ref, ref, (cb_send, cb_recv), far, me, 1 - core)
 
-    split[0], split[1] = split_two(design_ref[...])
     first_row = me * length
     lane = lax.broadcasted_iota(jnp.int32, (LANES, LANES), 1)
     step_rows = min(tile, 256)
@@ -125,11 +137,18 @@
                 blocks.append(entry.astype(jnp.float32).astype(jnp.bfloat16))
             stacked.append(jnp.concatenate(blocks, axis=1))
         table = jnp.concatenate(stacked, axis=0)
+        if far == high - 1 and start == 0:
+            for index in range(LOADS):
+                loads[2 + index].wait()
+                piece = slice(index * chunk, (index + 1) * chunk)
+                split[0, piece], split[1, piece] = split_two(design_ref[piece])
         total = jnp.dot(table, split[1], preferred_element_type=jnp.float32)
         total += jnp.dot(table, split[0], preferred_element_type=jnp.float32)
         owner = start // per
         buf[far, owner : owner + step_rows // per] = (total * scale).reshape(step_rows // per, per, width)
 
+    loads[0].wait()
+    loads[1].wait()
     for far in fars + [0]:
         for start in range(0, tile, step_rows):
             transform_rows(far, start)
@@ -248,15 +267,20 @@
     for shape in ((high, low), (high,), (high,), (low,), (high,), (high, low), (low,), (high,), (high, low), (high,)):
         sems += [pltpu.SemaphoreType.DMA(shape)] * 2
     late = per - early
+    limit = min(60 * 1024 * 1024, 4 * (7 * count * width + 3 * length * width + whole * whole) + 12 * 1024 * 1024)
     return pl.pallas_call(
         functools.partial(sketch_kernel, low, 1.0 / math.sqrt(length * n), early),
         out_shape=(
             jax.ShapeDtypeStruct((per, width), jnp.float32),
             jax.ShapeDtypeStruct((whole, whole), jnp.float32),
         ),
-        in_specs=[pl.BlockSpec(memory_space=pltpu.VMEM)] * 3,
+        in_specs=[pl.BlockSpec(memory_space=pltpu.HBM)] * 3,
         out_specs=(pl.BlockSpec(memory_space=pltpu.VMEM),) * 2,
         scratch_shapes=[
+            pltpu.VMEM((length, width), jnp.float32),
+            pltpu.VMEM((length // LANES, LANES), jnp.int32),
+            pltpu.VMEM((count // LANES, LANES), jnp.int32),
+            pltpu.SemaphoreType.DMA((2 + LOADS,)),
             pltpu.VMEM((2, length, width), jnp.bfloat16),
             pltpu.VMEM((high, low, per, width), jnp.float32),
             pltpu.VMEM((high, low, early, width), jnp.float32),
@@ -269,9 +293,9 @@
             *sems,
         ],
         compiler_params=pltpu.CompilerParams(
-            collective_id=0, has_side_effects=True, vmem_limit_bytes=60 * 1024 * 1024
+            collective_id=0, has_side_effects=True, vmem_limit_bytes=limit
         ),
-    )(design, signs.reshape(-1, LANES), kept.reshape(-1, LANES))
+    )(*(pltpu.with_memory_space_constraint(x, pltpu.HBM) for x in (design, signs.reshape(-1, LANES), kept.reshape(-1, LANES))))
 
 
 def spread(x, lane):
@@ -309,46 +333,74 @@
         done.append(top)
     return done
 
-def cholesky_kernel(scale, panel, gram_ref, out_ref, work, upper):
+def cholesky_kernel(scale, panel, gram_ref, sketch_ref, sketch_hbm, out_hbm, work, upper, sems):
     size = gram_ref.shape[0]
+    width = out_hbm.shape[1]
     tiles = size // LANES
     depth = panel // 8
+    lanes = pl.ds(pl.multiple_of(lax.axis_index("cols") * width, width), width)
+    copies = [pltpu.make_async_copy(sketch_ref, sketch_hbm, sems.at[size // panel])]
+    copies[0].start()
     work[...] = gram_ref[...] * scale
-    upper[...] = jnp.zeros_like(upper)
     dims = (((0,), (0,)), ((), ()))
     for start in range(0, size, panel):
-        t0 = start // LANES
-        first = start - t0 * LANES
-        rows = [[work[start + 8*r : start + 8*r + 8, t*LANES:(t+1)*LANES] for t in range(t0, tiles)] for r in range(depth)]
+        base = start // LANES
+        first = start - base * LANES
+        rows = [
+            [
+                work[start + 8 * r : start + 8 * r + 8, t * LANES : (t + 1) * LANES]
+                for t in range(base, tiles)
+            ]
+            for r in range(depth)
+        ]
         done = factor_panel(rows, first)
         full = jnp.concatenate([jnp.concatenate(d, axis=1) for d in done], axis=0)
         row = lax.broadcasted_iota(jnp.int32, full.shape, 0) + first
-        col = lax.broadcasted_iota(jnp.int32, full.shape, 1)
-        full = jnp.where(row <= col, full, 0.0)
-        upper[start:start+panel, t0*LANES:] = full
+        column = lax.broadcasted_iota(jnp.int32, full.shape, 1)
+        full = jnp.where(row <= column, full, 0.0)
         stop = start + panel
-        if stop == size: break
+        if base:
+            upper[start:stop, : base * LANES] = jnp.zeros((panel, base * LANES), jnp.float32)
+        upper[start:stop, base * LANES :] = full
+        copies.append(
+            pltpu.make_async_copy(
+                upper.at[start:stop, lanes], out_hbm.at[start:stop], sems.at[start // panel]
+            )
+        )
+        copies[-1].start()
+        if stop == size:
+            break
         high, low = split_two(full)
         left = jnp.concatenate([high, high, low], axis=0)
         right = jnp.concatenate([high, low, high], axis=0)
         for t in range(stop // LANES, tiles):
-            lo = max(stop, t * LANES)
-            off = (t - t0) * LANES
-            prod = lax.dot_general(left[:, off:off+LANES], right[:, off:], dims, preferred_element_type=jnp.float32)
-            work[lo:(t+1)*LANES, t*LANES:] -= prod[lo - t*LANES:]
-    width = out_ref.shape[1]
-    if width == size: out_ref[...] = upper[...]
-    else: out_ref[...] = upper[:, pl.ds(pl.multiple_of(lax.axis_index("cols") * width, width), width)]
-
-def cholesky(gram, scale, width, panel=32):
+            begin = max(stop, t * LANES)
+            offset = (t - base) * LANES
+            product = lax.dot_general(
+                left[:, offset : offset + LANES], right[:, offset:], dims, preferred_element_type=jnp.float32
+            )
+            work[begin : (t + 1) * LANES, t * LANES :] -= product[begin - t * LANES :]
+    for copy in copies:
+        copy.wait()
+
+
+def cholesky(gram, sketch, scale, width, panel=32):
     size = gram.shape[0]
     return pl.pallas_call(
         functools.partial(cholesky_kernel, scale, panel),
-        out_shape=jax.ShapeDtypeStruct((size, width), jnp.float32),
-        in_specs=[pl.BlockSpec(memory_space=pltpu.VMEM)],
-        out_specs=pl.BlockSpec(memory_space=pltpu.VMEM),
-        scratch_shapes=[pltpu.VMEM((size, size), jnp.float32)] * 2,
-    )(gram)
+        out_shape=(
+            jax.ShapeDtypeStruct(sketch.shape, jnp.float32),
+            jax.ShapeDtypeStruct((size, width), jnp.float32),
+        ),
+        in_specs=[pl.BlockSpec(memory_space=pltpu.VMEM)] * 2,
+        out_specs=(pl.BlockSpec(memory_space=pltpu.HBM),) * 2,
+        scratch_shapes=[
+            pltpu.VMEM((size, size), jnp.float32),
+            pltpu.VMEM((size, size), jnp.float32),
+            pltpu.SemaphoreType.DMA((size // panel + 1,)),
+        ],
+        compiler_params=pltpu.CompilerParams(vmem_limit_bytes=16 * 1024 * 1024),
+    )(gram, sketch)
 
 
 def solution(mesh):
@@ -356,7 +408,7 @@
 
     def body(design, signs, kept):
         sketch, gram = sketch_and_gram(design, signs, kept, n, cores)
-        return (sketch, cholesky(gram, 1.0 / kept.shape[0], design.shape[1]))
+        return cholesky(gram, sketch, 1.0 / kept.shape[0], design.shape[1])
 
     return jax.shard_map(
         body,

time: 52 us -> 46.7 us (0.90); the launches traced: 51.2 us -> 46.5 us
  Pallas kernels: 49.9 us -> 45.9 us
  local copies, waits for them, and re-layouts: 0.63 us -> 0 us
    pallas_call x1, Pallas kernels: 36.6 us -> 33.9 us  [sketch_and_gram(): pl.pallas_call(functools.partial(sketch_kernel, low, 1.0 / math.sqrt(leng...]
    pallas_call x1, Pallas kernels: 13.3 us -> 12 us  [cholesky(): pl.pallas_call(functools.partial(cholesky_kernel, scale, panel), out_shap...]
    unnamed x3 -> x0, local copies, waits for them, and re-layouts: 0.63 us -> none
where the time goes in v3:
time: 46.7 us; the launch traced here: 46.5 us
  Pallas kernels  45.9 us (98%)
  between operations  0.64 us (1%)
    pallas_call x1, Pallas kernels, sketch_and_gram(): pl.pallas_call(functools.partial(sketch_kernel, low, 1.0 / math.sqrt(leng...  33.9 us
    pallas_call x1, Pallas kernels, cholesky(): pl.pallas_call(functools.partial(cholesky_kernel, scale, panel), out_shap...  12 us

profile of v3, /device:TPU:0, one launch (start us, length us, event | category | flops | bytes accessed | tf_op | source)
XLA Modules:
  0.0 46.5 jit_solution(1463011017647482771)
XLA Ops:
  0.6 33.9 %shard_map.50 = (f32[64,256]{1,0:T(8,128)S(1)}, f32[512,512]{1,0:T(8,128)S(1)}) custom-call(f32[1024,256]{1,0:T(8,128)} %design_hbm.1, s32[8,128]{1,0:T(8,128)} %bitcast.2, s32[8,128]{1,0:T(8,128)} %bitcast.3), custom_call_target="tpu_custom_call" | custom-call | tf_op jit(solution)/shard_map/pallas_call | solution.py:271
  34.5 12.0 %shard_map.51 = (f32[64,256]{1,0:T(8,128)}, f32[512,256]{1,0:T(8,128)}) custom-call(f32[512,512]{1,0:T(8,128)S(1)} %get-tuple-element.4.gram_ref, f32[64,256]{1,0:T(8,128)S(1)} %get-tuple-element.5.sketch_ref), custom_call_target="tpu_custom_call" | custom-call | tf_op jit(solution)/shard_map/pallas_call | solution.py:389

commit v4 on v3

--- a/solution.py
+++ b/solution.py
@@ -19,12 +19,11 @@
 
 
 def sketch_kernel(
-    low, scale, early,
+    low, scale, early, gathers,
     design_hbm, signs_hbm, kept_hbm, sketch_ref, gram_ref,
     design_ref, signs_ref, kept_ref, load_sems, split, buf, one_a, one_b, out_a, out_b, two_a, two_b, gat,
     one_a_send, one_a_recv, one_b_send, one_b_recv, two_a_send, two_a_recv, two_b_send, two_b_recv,
-    az_send, az_recv, axy_send, axy_recv, bxy_send, bxy_recv, bz_send, bz_recv,
-    ca_send, ca_recv, cb_send, cb_recv,
+    far_send, far_recv, near_send, near_recv, core_send, core_recv,
 ):
     me = lax.axis_index("rows")
     core = lax.axis_index("cols")
@@ -70,6 +69,7 @@
 
     nears = list(range(low - 1, 0, -1))
     fars = list(range(high - 1, 0, -1))
+    closest = sorted(fars, key=lambda far: far > 1)
 
     barrier = pltpu.get_barrier_semaphore()
     for near in nears:
@@ -95,29 +95,50 @@
             out_b.at[flip(spot, near)], two_b.at[near], (two_b_send, two_b_recv), near, peer(near, 0)
         )
 
-    def az_copy(far):
-        ref = gat.at[me, head, lanes]
-        return send(ref, ref, (az_send, az_recv), far, peer(0, far))
-
-    def axy_copy(far, near):
-        ref = gat.at[peer(0, far), head, lanes]
-        return send(ref, ref, (axy_send, axy_recv), (far, near), peer(near, 0))
-
-    def bxy_copy(near):
-        ref = gat.at[me, tail, lanes]
-        return send(ref, ref, (bxy_send, bxy_recv), near, peer(near, 0))
-
-    def bz_copy(far):
-        ref = gat.at[pl.ds((me // low) * low, low), tail, lanes]
-        return send(ref, ref, (bz_send, bz_recv), far, peer(0, far))
-
-    def ca_copy(far, near):
-        ref = gat.at[peer(near, far), head, lanes]
-        return send(ref, ref, (ca_send, ca_recv), (far, near), me, 1 - core)
-
-    def cb_copy(far):
-        ref = gat.at[pl.ds(plane(far) * low, low), tail, lanes]
-        return send(ref, ref, (cb_send, cb_recv), far, me, 1 - core)
+    def rows_of(part):
+        return pl.ds(gathers[part][1], gathers[part][2])
+
+    def near_copy(part, far, near):
+        ref = gat.at[peer(0, far), rows_of(part), lanes]
+        return send(ref, ref, (near_send, near_recv), (part, far, near), peer(near, 0))
+
+    def far_copy(part, far):
+        if gathers[part][0]:
+            ref = gat.at[me, rows_of(part), lanes]
+        else:
+            ref = gat.at[pl.ds((me // low) * low, low), rows_of(part), lanes]
+        return send(ref, ref, (far_send, far_recv), (part, far), peer(0, far))
+
+    def core_copy(part, far):
+        ref = gat.at[pl.ds(plane(far) * low, low), rows_of(part), lanes]
+        return send(ref, ref, (core_send, core_recv), (part, far), me, 1 - core)
+
+    def begin(part):
+        if gathers[part][0]:
+            for far in closest:
+                far_copy(part, far).start()
+        for near in nears:
+            near_copy(part, 0, near).start()
+
+    def middle(part, far):
+        if gathers[part][0]:
+            far_copy(part, far).wait_recv()
+            for near in nears:
+                near_copy(part, far, near).start()
+        else:
+            for near in nears:
+                near_copy(part, 0, near).wait_recv()
+            for other in fars:
+                far_copy(part, other).start()
+            core_copy(part, 0).start()
+
+    def finish(part, far):
+        if gathers[part][0]:
+            for near in nears:
+                near_copy(part, far, near).wait_recv()
+        else:
+            far_copy(part, far).wait_recv()
+        core_copy(part, far).start()
 
     first_row = me * length
     lane = lax.broadcasted_iota(jnp.int32, (LANES, LANES), 1)
@@ -182,24 +203,20 @@
         total += two_a[far]
     sketch_ref[head, :] = total
     gat[me, head, lanes] = total
-    for far in fars:
-        az_copy(far).start()
-    for near in nears:
-        axy_copy(0, near).start()
-    ca_copy(0, 0).start()
+    for part in [part for part in range(len(gathers)) if gathers[part][1] < early]:
+        begin(part)
     total = out_b[spot]
     for near in nears:
         two_b_copy(near).wait_recv()
         total += two_b[near]
     sketch_ref[tail, :] = total
     gat[me, tail, lanes] = total
-    for near in nears:
-        bxy_copy(near).start()
+    for part in [part for part in range(len(gathers)) if gathers[part][1] >= early]:
+        begin(part)
 
     def add_gram(far, first):
-        for near in range(low):
-            ca_copy(far, near).wait_recv()
-        cb_copy(far).wait_recv()
+        for part in range(len(gathers)):
+            core_copy(part, far).wait_recv()
         half = whole // 2
         rows = gat[pl.ds(plane(far) * low, low)].reshape(tile, whole)
         upper, rest = split_two(rows)
@@ -211,44 +228,39 @@
         gram_ref[0:half, :] = a if first else gram_ref[0:half, :] + a
         gram_ref[half:, half:] = c if first else gram_ref[half:, half:] + c
 
-    for near in nears:
-        bxy_copy(near).wait_recv()
-    for far in fars:
-        bz_copy(far).start()
-    cb_copy(0).start()
-    for near in nears:
-        axy_copy(0, near).wait_recv()
-        ca_copy(0, near).start()
-    for far in fars:
-        az_copy(far).wait_recv()
+    passed = [part for part in range(len(gathers)) if gathers[part][0]]
+    for part in range(len(gathers)):
+        if part not in passed:
+            middle(part, 0)
+    for index, far in enumerate(closest):
+        for part in passed:
+            middle(part, far)
+            if index == 0:
+                finish(part, 0)
+    gram_ref[half_rows(gram_ref) :, : whole // 2] = jnp.zeros((whole // 2, whole // 2), jnp.float32)
+    ready = 0
+    for far in closest:
+        for part in range(len(gathers)):
+            finish(part, far)
+        add_gram(ready, ready == 0)
+        ready = far
+    add_gram(ready, ready == 0)
+
+    for far in range(high):
         for near in nears:
-            axy_copy(far, near).start()
-        ca_copy(far, 0).start()
-    gram_ref[half_rows(gram_ref) :, : whole // 2] = jnp.zeros((whole // 2, whole // 2), jnp.float32)
-    add_gram(0, True)
-    for far in fars:
-        for near in nears:
-            axy_copy(far, near).wait_recv()
-            ca_copy(far, near).start()
-        bz_copy(far).wait_recv()
-        cb_copy(far).start()
-        add_gram(far, False)
-
-    for far in range(high):
-        for near in range(low):
-            if near:
-                one_a_copy(far, near).wait_send()
-                axy_copy(far, near).wait_send()
-            ca_copy(far, near).wait_send()
-        cb_copy(far).wait_send()
+            one_a_copy(far, near).wait_send()
         if far:
             one_b_copy(far).wait_send()
             two_a_copy(far).wait_send()
-            az_copy(far).wait_send()
-            bz_copy(far).wait_send()
+        for part in range(len(gathers)):
+            core_copy(part, far).wait_send()
+            if far:
+                far_copy(part, far).wait_send()
+            if gathers[part][0] or far == 0:
+                for near in nears:
+                    near_copy(part, far, near).wait_send()
     for near in nears:
         two_b_copy(near).wait_send()
-        bxy_copy(near).wait_send()
 
 
 def half_rows(ref):
@@ -262,14 +274,17 @@
     low = 1 << ((n.bit_length() - 1) // 2)
     high = n // low
     early = per - per // 4
+    eighth = per // 8
+    gathers = ((0, 0, eighth), (1, eighth, early - eighth), (1, early, per - early))
     whole = width * cores
     sems = []
-    for shape in ((high, low), (high,), (high,), (low,), (high,), (high, low), (low,), (high,), (high, low), (high,)):
+    count_g = len(gathers)
+    for shape in ((high, low), (high,), (high,), (low,), (count_g, high), (count_g, high, low), (count_g, high)):
         sems += [pltpu.SemaphoreType.DMA(shape)] * 2
     late = per - early
     limit = min(60 * 1024 * 1024, 4 * (7 * count * width + 3 * length * width + whole * whole) + 12 * 1024 * 1024)
     return pl.pallas_call(
-        functools.partial(sketch_kernel, low, 1.0 / math.sqrt(length * n), early),
+        functools.partial(sketch_kernel, low, 1.0 / math.sqrt(length * n), early, gathers),
         out_shape=(
             jax.ShapeDtypeStruct((per, width), jnp.float32),
             jax.ShapeDtypeStruct((whole, whole), jnp.float32),
@@ -301,39 +316,41 @@
 def spread(x, lane):
     return jnp.broadcast_to(x[:, lane:lane+1], x.shape)
 
-def factor_panel(rows, first):
+def factor_panel(rows, first, reach):
     depth = len(rows)
-    tiles = len(rows[0])
+    size = 8 * depth
     sub = lax.broadcasted_iota(jnp.int32, (8, LANES), 0)
     rows = [list(r) for r in rows]
-    ahead = [[spread(rows[r][0], first + j) for r in range(depth)] for j in range(8)]
-    done = []
-    for g in range(depth):
-        here = ahead
-        if g + 1 < depth:
-            ahead = [[spread(rows[r][0], first + 8 * (g + 1) + j) for r in range(g + 1, depth)] for j in range(8)]
-        top = rows[g]
-        for j in range(8):
-            column = here[j]
-            root = lax.rsqrt(column[0][j:j+1])
-            root = jnp.broadcast_to(root, (8, LANES))
-            scaled = [c * root for c in column]
-            for later in range(j + 1, 8):
-                weight = here[later][0][j:j+1] * root
-                here[later] = [c - s * weight for c, s in zip(here[later], scaled)]
-            below = jnp.where(sub > j, scaled[0], 0.0)
-            lines = [t[j:j+1] * root for t in top]
-            top = [jnp.where(sub == j, l, t - below * l) for t, l in zip(top, lines)]
-            for r in range(g + 1, depth):
-                rows[r] = [x - scaled[r - g] * l for x, l in zip(rows[r], lines)]
-            if g + 1 < depth:
-                for l in range(8):
-                    weight = scaled[1][l:l+1]
-                    ahead[l] = [c - s * weight for c, s in zip(ahead[l], scaled[1:])]
-        done.append(top)
-    return done
-
-def cholesky_kernel(scale, panel, gram_ref, sketch_ref, sketch_hbm, out_hbm, work, upper, sems):
+    columns = {}
+
+    def fetch(j):
+        if j < size:
+            columns[j] = [spread(rows[r][0], first + j) for r in range(j // 8, depth)]
+
+    for j in range(reach + 1):
+        fetch(j)
+    for i in range(size):
+        g, j = i // 8, i % 8
+        column = columns.pop(i)
+        root = jnp.broadcast_to(lax.rsqrt(column[0][j : j + 1]), (8, LANES))
+        scaled = [c * root for c in column]
+        for later in range(i + 1, min(i + reach, size - 1) + 1):
+            q = later // 8
+            if q == g and later == i + 1:
+                weight = columns[later][0][j : j + 1] * root
+            else:
+                weight = scaled[q - g][later % 8 : later % 8 + 1]
+            columns[later] = [c - s * weight for c, s in zip(columns[later], scaled[q - g :])]
+        below = jnp.where(sub > j, scaled[0], 0.0)
+        lines = [t[j : j + 1] * root for t in rows[g]]
+        rows[g] = [jnp.where(sub == j, l, t - below * l) for t, l in zip(rows[g], lines)]
+        for r in range(g + 1, depth):
+            rows[r] = [x - scaled[r - g] * l for x, l in zip(rows[r], lines)]
+        fetch(i + reach + 1)
+    return rows
+
+
+def cholesky_kernel(scale, panel, reach, gram_ref, sketch_ref, sketch_hbm, out_hbm, work, upper, sems):
     size = gram_ref.shape[0]
     width = out_hbm.shape[1]
     tiles = size // LANES
@@ -353,7 +370,7 @@
             ]
             for r in range(depth)
         ]
-        done = factor_panel(rows, first)
+        done = factor_panel(rows, first, reach)
         full = jnp.concatenate([jnp.concatenate(d, axis=1) for d in done], axis=0)
         row = lax.broadcasted_iota(jnp.int32, full.shape, 0) + first
         column = lax.broadcasted_iota(jnp.int32, full.shape, 1)
@@ -384,10 +401,10 @@
         copy.wait()
 
 
-def cholesky(gram, sketch, scale, width, panel=32):
+def cholesky(gram, sketch, scale, width, panel=32, reach=12):
     size = gram.shape[0]
     return pl.pallas_call(
-        functools.partial(cholesky_kernel, scale, panel),
+        functools.partial(cholesky_kernel, scale, panel, reach),
         out_shape=(
             jax.ShapeDtypeStruct(sketch.shape, jnp.float32),
             jax.ShapeDtypeStruct((size, width), jnp.float32),

time: 46.7 us -> 45.1 us (0.966)
  Pallas kernels: 45.9 us -> 44 us
    pallas_call x1, Pallas kernels: 33.9 us -> 32.4 us  [sketch_and_gram(): pl.pallas_call(functools.partial(sketch_kernel, low, 1.0 / math.sqrt(leng...]
where the time goes in v4:
time: 45.1 us; the launch traced here: 44.7 us
  Pallas kernels  44 us (98%)
  between operations  0.64 us (1%)
    pallas_call x1, Pallas kernels, sketch_and_gram(): pl.pallas_call(functools.partial(sketch_kernel, low, 1.0 / math.sqrt(leng...  32.4 us
    pallas_call x1, Pallas kernels, cholesky(): pl.pallas_call(functools.partial(cholesky_kernel, scale, panel, reach), o...  11.6 us

profile of v4, /device:TPU:0, one launch (start us, length us, event | category | flops | bytes accessed | tf_op | source)
XLA Modules:
  0.0 44.7 jit_solution(6409066744555350222)
XLA Ops:
  0.6 32.4 %shard_map.50 = (f32[64,256]{1,0:T(8,128)S(1)}, f32[512,512]{1,0:T(8,128)S(1)}) custom-call(f32[1024,256]{1,0:T(8,128)} %design_hbm.1, s32[8,128]{1,0:T(8,128)} %bitcast.2, s32[8,128]{1,0:T(8,128)} %bitcast.3), custom_call_target="tpu_custom_call" | custom-call | tf_op jit(solution)/shard_map/pallas_call | solution.py:286
  33.1 11.6 %shard_map.51 = (f32[64,256]{1,0:T(8,128)}, f32[512,256]{1,0:T(8,128)}) custom-call(f32[512,512]{1,0:T(8,128)S(1)} %get-tuple-element.4.gram_ref, f32[64,256]{1,0:T(8,128)S(1)} %get-tuple-element.5.sketch_ref), custom_call_target="tpu_custom_call" | custom-call | tf_op jit(solution)/shard_map/pallas_call | solution.py:406

commit v5 on v4

--- a/solution.py
+++ b/solution.py
@@ -42,9 +42,7 @@
         load.start()
     length = design_ref.shape[0]
     tile = low * per
-    whole = gat.shape[2]
     spot = me % low
-    lanes = pl.ds(pl.multiple_of(core * width, LANES), width)
     head, tail = pl.ds(0, early), pl.ds(early, per - early)
 
     def flip(value, mask):
@@ -99,18 +97,18 @@
         return pl.ds(gathers[part][1], gathers[part][2])
 
     def near_copy(part, far, near):
-        ref = gat.at[peer(0, far), rows_of(part), lanes]
+        ref = gat.at[core, peer(0, far), rows_of(part)]
         return send(ref, ref, (near_send, near_recv), (part, far, near), peer(near, 0))
 
     def far_copy(part, far):
         if gathers[part][0]:
-            ref = gat.at[me, rows_of(part), lanes]
+            ref = gat.at[core, me, rows_of(part)]
         else:
-            ref = gat.at[pl.ds((me // low) * low, low), rows_of(part), lanes]
+            ref = gat.at[core, pl.ds((me // low) * low, low), rows_of(part)]
         return send(ref, ref, (far_send, far_recv), (part, far), peer(0, far))
 
     def core_copy(part, far):
-        ref = gat.at[pl.ds(plane(far) * low, low), rows_of(part), lanes]
+        ref = gat.at[core, pl.ds(plane(far) * low, low), rows_of(part)]
         return send(ref, ref, (core_send, core_recv), (part, far), me, 1 - core)
 
     def begin(part):
@@ -128,7 +126,7 @@
         else:
             for near in nears:
                 near_copy(part, 0, near).wait_recv()
-            for other in fars:
+            for other in closest:
                 far_copy(part, other).start()
             core_copy(part, 0).start()
 
@@ -158,7 +156,7 @@
                 blocks.append(entry.astype(jnp.float32).astype(jnp.bfloat16))
             stacked.append(jnp.concatenate(blocks, axis=1))
         table = jnp.concatenate(stacked, axis=0)
-        if far == high - 1 and start == 0:
+        if far == fars[0] and start == 0:
             for index in range(LOADS):
                 loads[2 + index].wait()
                 piece = slice(index * chunk, (index + 1) * chunk)
@@ -173,7 +171,7 @@
     for far in fars + [0]:
         for start in range(0, tile, step_rows):
             transform_rows(far, start)
-        if far == high - 1:
+        if far == fars[0]:
             pl.semaphore_wait(barrier, len(nears) + len(fars) + 1)
         for near in nears:
             one_a_copy(far, near).start()
@@ -202,7 +200,7 @@
         two_a_copy(far).wait_recv()
         total += two_a[far]
     sketch_ref[head, :] = total
-    gat[me, head, lanes] = total
+    gat[core, me, head] = total
     for part in [part for part in range(len(gathers)) if gathers[part][1] < early]:
         begin(part)
     total = out_b[spot]
@@ -210,15 +208,16 @@
         two_b_copy(near).wait_recv()
         total += two_b[near]
     sketch_ref[tail, :] = total
-    gat[me, tail, lanes] = total
+    gat[core, me, tail] = total
     for part in [part for part in range(len(gathers)) if gathers[part][1] >= early]:
         begin(part)
 
     def add_gram(far, first):
         for part in range(len(gathers)):
             core_copy(part, far).wait_recv()
-        half = whole // 2
-        rows = gat[pl.ds(plane(far) * low, low)].reshape(tile, whole)
+        owners = pl.ds(plane(far) * low, low)
+        rows = jnp.concatenate([gat[side, owners].reshape(tile, width) for side in range(gat.shape[0])], axis=1)
+        half = rows.shape[1] // 2
         upper, rest = split_two(rows)
         left = jnp.concatenate([upper, upper, rest], axis=0)
         right = jnp.concatenate([upper, rest, upper], axis=0)
@@ -229,15 +228,15 @@
         gram_ref[half:, half:] = c if first else gram_ref[half:, half:] + c
 
     passed = [part for part in range(len(gathers)) if gathers[part][0]]
-    for part in range(len(gathers)):
-        if part not in passed:
-            middle(part, 0)
     for index, far in enumerate(closest):
         for part in passed:
             middle(part, far)
             if index == 0:
                 finish(part, 0)
-    gram_ref[half_rows(gram_ref) :, : whole // 2] = jnp.zeros((whole // 2, whole // 2), jnp.float32)
+                if part == passed[0]:
+                    for other in range(len(gathers)):
+                        if other not in passed:
+                            middle(other, 0)
     ready = 0
     for far in closest:
         for part in range(len(gathers)):
@@ -261,10 +260,6 @@
                     near_copy(part, far, near).wait_send()
     for near in nears:
         two_b_copy(near).wait_send()
-
-
-def half_rows(ref):
-    return ref.shape[0] // 2
 
 
 def sketch_and_gram(design, signs, kept, n, cores):
@@ -304,7 +299,7 @@
             pltpu.VMEM((low, late, width), jnp.float32),
             pltpu.VMEM((high, early, width), jnp.float32),
             pltpu.VMEM((low, late, width), jnp.float32),
-            pltpu.VMEM((n, per, whole), jnp.float32),
+            pltpu.VMEM((cores, n, per, width), jnp.float32),
             *sems,
         ],
         compiler_params=pltpu.CompilerParams(
@@ -332,7 +327,7 @@
     for i in range(size):
         g, j = i // 8, i % 8
         column = columns.pop(i)
-        root = jnp.broadcast_to(lax.rsqrt(column[0][j : j + 1]), (8, LANES))
+        root = jnp.broadcast_to(lax.rsqrt(column[0])[j : j + 1], (8, LANES))
         scaled = [c * root for c in column]
         for later in range(i + 1, min(i + reach, size - 1) + 1):
             q = later // 8
@@ -358,14 +353,14 @@
     lanes = pl.ds(pl.multiple_of(lax.axis_index("cols") * width, width), width)
     copies = [pltpu.make_async_copy(sketch_ref, sketch_hbm, sems.at[size // panel])]
     copies[0].start()
-    work[...] = gram_ref[...] * scale
     dims = (((0,), (0,)), ((), ()))
     for start in range(0, size, panel):
         base = start // LANES
         first = start - base * LANES
+        source = work if start else gram_ref
         rows = [
             [
-                work[start + 8 * r : start + 8 * r + 8, t * LANES : (t + 1) * LANES]
+                source[start + 8 * r : start + 8 * r + 8, t * LANES : (t + 1) * LANES]
                 for t in range(base, tiles)
             ]
             for r in range(depth)
@@ -378,7 +373,7 @@
         stop = start + panel
         if base:
             upper[start:stop, : base * LANES] = jnp.zeros((panel, base * LANES), jnp.float32)
-        upper[start:stop, base * LANES :] = full
+        upper[start:stop, base * LANES :] = full * math.sqrt(scale)
         copies.append(
             pltpu.make_async_copy(
                 upper.at[start:stop, lanes], out_hbm.at[start:stop], sems.at[start // panel]
@@ -396,7 +391,8 @@
             product = lax.dot_general(
                 left[:, offset : offset + LANES], right[:, offset:], dims, preferred_element_type=jnp.float32
             )
-            work[begin : (t + 1) * LANES, t * LANES :] -= product[begin - t * LANES :]
+            place = (slice(begin, (t + 1) * LANES), slice(t * LANES, size))
+            work[place] = source[place] - product[begin - t * LANES :]
     for copy in copies:
         copy.wait()
 

time: 45.1 us -> 44.9 us (level)
  no operation moved by 1% of the time
where the time goes in v5:
time: 44.9 us; the launch traced here: 44.5 us
  Pallas kernels  43.8 us (98%)
  between operations  0.64 us (1%)
    pallas_call x1, Pallas kernels, sketch_and_gram(): pl.pallas_call(functools.partial(sketch_kernel, low, 1.0 / math.sqrt(leng...  32.2 us
    pallas_call x1, Pallas kernels, cholesky(): pl.pallas_call(functools.partial(cholesky_kernel, scale, panel, reach), o...  11.6 us

profile of v5, /device:TPU:0, one launch (start us, length us, event | category | flops | bytes accessed | tf_op | source)
XLA Modules:
  0.0 44.5 jit_solution(13650064802945677572)
XLA Ops:
  0.6 32.2 %shard_map.50 = (f32[64,256]{1,0:T(8,128)S(1)}, f32[512,512]{1,0:T(8,128)S(1)}) custom-call(f32[1024,256]{1,0:T(8,128)} %design_hbm.1, s32[8,128]{1,0:T(8,128)} %bitcast.2, s32[8,128]{1,0:T(8,128)} %bitcast.3), custom_call_target="tpu_custom_call" | custom-call | tf_op jit(solution)/shard_map/pallas_call | solution.py:281
  32.8 11.6 %shard_map.51 = (f32[64,256]{1,0:T(8,128)}, f32[512,256]{1,0:T(8,128)}) custom-call(f32[512,512]{1,0:T(8,128)S(1)} %get-tuple-element.4.gram_ref, f32[64,256]{1,0:T(8,128)S(1)} %get-tuple-element.5.sketch_ref), custom_call_target="tpu_custom_call" | custom-call | tf_op jit(solution)/shard_map/pallas_call | solution.py:402

commit v6 on v5

--- a/solution.py
+++ b/solution.py
@@ -239,7 +239,7 @@
                             middle(other, 0)
     ready = 0
     for far in closest:
-        for part in range(len(gathers)):
+        for part in sorted(range(len(gathers)), key=lambda part: part not in passed):
             finish(part, far)
         add_gram(ready, ready == 0)
         ready = far

time: 44.9 us -> 44.9 us (level)
  no operation moved by 1% of the time
where the time goes in v6:
time: 44.9 us; the launch traced here: 44.5 us
  Pallas kernels  43.8 us (98%)
  between operations  0.64 us (1%)
    pallas_call x1, Pallas kernels, sketch_and_gram(): pl.pallas_call(functools.partial(sketch_kernel, low, 1.0 / math.sqrt(leng...  32.2 us
    pallas_call x1, Pallas kernels, cholesky(): pl.pallas_call(functools.partial(cholesky_kernel, scale, panel, reach), o...  11.6 us

profile of v6, /device:TPU:0, one launch (start us, length us, event | category | flops | bytes accessed | tf_op | source)
XLA Modules:
  0.0 44.5 jit_solution(8191116964788334234)
XLA Ops:
  0.6 32.2 %shard_map.50 = (f32[64,256]{1,0:T(8,128)S(1)}, f32[512,512]{1,0:T(8,128)S(1)}) custom-call(f32[1024,256]{1,0:T(8,128)} %design_hbm.1, s32[8,128]{1,0:T(8,128)} %bitcast.2, s32[8,128]{1,0:T(8,128)} %bitcast.3), custom_call_target="tpu_custom_call" | custom-call | tf_op jit(solution)/shard_map/pallas_call | solution.py:281
  32.8 11.6 %shard_map.51 = (f32[64,256]{1,0:T(8,128)}, f32[512,256]{1,0:T(8,128)}) custom-call(f32[512,512]{1,0:T(8,128)S(1)} %get-tuple-element.4.gram_ref, f32[64,256]{1,0:T(8,128)S(1)} %get-tuple-element.5.sketch_ref), custom_call_target="tpu_custom_call" | custom-call | tf_op jit(solution)/shard_map/pallas_call | solution.py:402
